TPU v7x, 256 devices: a whole 4x4x8 slice. The times are simulated.
256 devices in a mesh: section: 32 (over y, z_lo, core), tensor: 8 (over z_hi, x).
Axes of the slice: x: 4, y: 4, z: 8 (z_hi: 2, z_lo: 4; z = z_hi * 4 + z_lo), core: 2. Of those that a mesh axis runs over, the one named last changes fastest.
Arguments:
- saved: bfloat16 [32, 32, 64, 8192], P('section', None, 'tensor'), may hold values from -6 to 6
- offsets: int32 [32, 32], P('section'), may hold values from 0 to 31, as said below
Outputs:
- restored: float32 [32, 32, 64, 8192], P('section', None, None, 'tensor')
- block_sums: float32 [32, 32, 8192], P('section', None, 'tensor')
Inputs may be any that keep to these rules, and one draw needn't show every extreme that they name: Each row of offsets is a permutation of 0 to 31.
All inputs are finite; a program needn't handle non-finite values.
Results may differ from a plain program's by a relative error of at most 0.0003.
Values may be sent and summed in bfloat16 or wider, within the bound.
A program may use at most 128 MiB of HBM per device.

v0:
```python
import jax
import jax.numpy as jnp
from jax import lax
from jax.sharding import PartitionSpec as P


def cut_along(array, dim, length):
    before, after = (array.shape[:dim], array.shape[dim + 1 :])
    return jnp.moveaxis(array.reshape(*before, length, -1, *after), dim, 0)


def laid_out(parts, dim):
    lengths = list(parts.shape[1:])
    lengths[dim] *= parts.shape[0]
    return jnp.moveaxis(parts, 0, dim).reshape(lengths)


def exchange_both(array, axis, axes, splits, concats):
    sizes = [lax.axis_size(a) for a in axes]
    parts = cut_along(array, splits[0], sizes[0])
    parts = jnp.moveaxis(cut_along(parts, splits[1] + 1, sizes[1]), 0, 1)
    inside = parts.shape[2:]
    parts = parts.reshape(-1, *inside)
    parts = lax.all_to_all(parts, axis, split_axis=0, concat_axis=0, tiled=True)
    parts = laid_out(parts.reshape(*sizes, *inside), concats[0] + 1)
    return laid_out(parts, concats[1])


def invert(table, count):
    return jnp.zeros((count,), jnp.int32).at[table].set(jnp.arange(count, dtype=jnp.int32))


def body(saved, offsets):
    count = lax.axis_size("section")
    mine = lax.axis_index("section")
    table = offsets[0]
    blocks = saved[0]
    order = invert((mine + table) % count, count)
    outgoing = jnp.take(blocks, order, axis=0)
    arrived = exchange_both(outgoing, ("section", "tensor"), ("section", "tensor"), (0, 2), (0, 1))
    restored = arrived.astype(jnp.float32)
    block_sums = jnp.sum(restored, axis=1)
    return (restored[None], block_sums[None])


def solution(mesh):
    return jax.shard_map(
        body,
        mesh=mesh,
        in_specs=(P("section", None, "tensor", None), P("section", None)),
        out_specs=(P("section", None, None, "tensor"), P("section", None, "tensor")),
        check_vma=False,
    )
```

profile of v0, /device:TPU:1, one launch (start us, length us, event | category | flops | bytes accessed | tf_op | source)
XLA Modules:
  0.0 131.5 jit_solution(2204318891240321854)
XLA Ops:
  0.6 0.7 fusion.1
  1.3 0.7 scatter_custom_fusion
  2.0 5.0 %gather_fusion = bf16[32,8,8192]{2,1,0:T(8,128)(2,1)} fusion(bf16[32,8,8192]{2,1,0:T(8,128)(2,1)} %bitcast.26, s32[1024]{0:T(1024)S(1)} %pad_clamp_fusion), kind=kCustom, calls=%fused_computation | custom fusion | bytes 8388736 | tf_op jit(solution)/shard_map/jit(_take)/gather | solution.py:39
  7.0 2.6 %broadcast_select_fusion = bf16[32,1,8,8,1024]{4,2,3,0,1:T(8,128)(2,1)S(1)} fusion(bf16[32,1,8,8,1024]{4,2,3,0,1:T(8,128)(2,1)} %bitcast.24, pred[32]{0:T(512)(128)(4,1)S(1)} %compare_and_fusion), kind=kLoop, calls=%fused_computation.2 | loop fusion | flops 2097152 | bytes 8388640 | tf_op jit(solution)/shard_map/jit(_take)/select_n | solution.py:39
  9.7 113.2 %all_to_all.5 = bf16[256,1,8,1024]{3,2,1,0:T(8,128)(2,1)S(1)} all-to-all(bf16[256,1,8,1024]{3,2,1,0:T(8,128)(2,1)S(1)} %bitcast.25), channel_id=1, replica_groups=mesh['section'=32,'tensor'=8] {'section','tensor'}, dimensions={0} | all-to-all | bytes 8388608 | tf_op jit(solution)/shard_map/all_to_all | solution.py:24
  122.9 3.2 %convert_reduce_fusion = f32[256,1024]{1,0:T(8,128)S(1)} fusion(bf16[256,1,8,1024]{3,2,1,0:T(8,128)(2,1)S(1)} %all_to_all.5), kind=kLoop, calls=%fused_computation.3 | loop fusion | flops 3932160 | bytes 5242880 | tf_op jit(solution)/shard_map/reduce_sum | solution.py:42
  126.1 0.9 bitcast_reduce_fusion
  127.0 4.5 %convert.5 = f32[1,32,64,1024]{3,2,1,0:T(8,128)} convert(bf16[1,32,64,1024]{3,2,1,0:T(8,128)(2,1)S(1)} %bitcast.23) | non-fusion elementwise | flops 2097152 | bytes 12582912 | tf_op jit(solution)/shard_map/convert_element_type | solution.py:41
  (4 shorter events, 0.0 us)
where the time goes:
time: 132 us; the launch traced here: 131 us
  blocking collectives  113 us (86%)
  other arithmetic  11.9 us (9%)
  local copies, waits for them, and re-layouts  5.69 us (4%)
    all_to_all x1, blocking collectives, exchange_both(): parts = lax.all_to_all(parts, axis, split_axis=0, concat_axis=0, tiled=True)  113 us
    gather x1, local copies, waits for them, and re-layouts, body(): outgoing = jnp.take(blocks, order, axis=0)  5.02 us
    convert_element_type x1, other arithmetic, body(): restored = arrived.astype(jnp.float32)  4.47 us
    reduce_sum x2, other arithmetic, body(): block_sums = jnp.sum(restored, axis=1)  4.12 us
    select_n x2, other arithmetic, body(): outgoing = jnp.take(blocks, order, axis=0)  2.65 us

commit v1 on v0

v1 whole, which is shorter than its diff:
```python
import jax
import jax.numpy as jnp
from jax import lax
from jax.experimental import pallas as pl
from jax.experimental.pallas import tpu as pltpu
from jax.sharding import PartitionSpec as P

MESH = pl.DeviceIdType.MESH
MIB = 1 << 20
FAR_FIRST = (2, 1, 3)
Z_ORDER = (4, 3, 5, 2, 6, 1, 7)


def exchange(saved, offsets, dst, raw, src, table, slot, load_sem, table_sem, send_sem, recv_sem, second, third):
    section, tensor = lax.axis_index("section"), lax.axis_index("tensor")
    y, z_lo, core = lax.div(section, 8), lax.rem(lax.div(section, 2), 4), lax.rem(section, 2)
    z_hi, x = lax.div(tensor, 4), lax.rem(tensor, 4)
    z = z_hi * 4 + z_lo

    def device(dx, dy, dz, dc):
        tx, ty, tz, tc = lax.rem(x + dx, 4), lax.rem(y + dy, 4), lax.rem(z + dz, 8), lax.rem(core + dc, 2)
        return (ty * 4 + lax.rem(tz, 4)) * 2 + tc, lax.div(tz, 4) * 4 + tx

    def signal(semaphore, *offset):
        pl.semaphore_signal(semaphore, inc=1, device_id=device(*offset), device_id_type=MESH)

    def send(*offset):
        to = device(*offset)
        columns = pl.ds(pl.multiple_of(to[1] * 1024, 1024), 1024)
        pltpu.make_async_remote_copy(
            src_ref=src.at[to[0], :, columns],
            dst_ref=dst.at[section * 8 + tensor],
            send_sem=send_sem,
            recv_sem=recv_sem,
            device_id=to,
            device_id_type=MESH,
        ).start()

    def loop(count, step):
        lax.fori_loop(0, count, lambda i, carry: (step(i), carry)[1], 0)

    barrier = pltpu.get_barrier_semaphore()
    for dz in Z_ORDER:
        signal(barrier, 0, 0, dz, 0)
    for d in FAR_FIRST:
        signal(barrier, 0, d, 0, 0)
        signal(barrier, d, 0, 0, 0)
    signal(barrier, 0, 0, 0, 1)

    read = pltpu.make_async_copy(offsets, table, table_sem)
    read.start()
    load = pltpu.make_async_copy(saved, raw, load_sem)
    load.start()
    read.wait()

    def find(t):
        wanted = lax.rem(t - section + 32, 32)
        found = jnp.int32(0)
        for j in range(32):
            found = jnp.where(table[0, j] == wanted, jnp.int32(j), found)
        slot[t] = found

    loop(32, find)
    load.wait()

    def place(t):
        src[t] = raw[slot[t]]

    loop(32, place)
    dst[section * 8 + tensor] = src[section, :, pl.ds(pl.multiple_of(tensor * 1024, 1024), 1024)]
    pl.semaphore_wait(barrier, 14)

    for d in FAR_FIRST:
        signal(second, 0, d, 0, 0)
        signal(second, d, 0, 0, 0)
    for dz in Z_ORDER:
        send(0, 0, dz, 0)
    for d in FAR_FIRST:
        send(0, d, 0, 0)
        send(d, 0, 0, 0)
    send(0, 0, 0, 1)
    pl.semaphore_wait(second, 6)

    for d in FAR_FIRST:
        signal(third, d, 0, 0, 1)
    signal(third, 0, 0, 0, 1)
    for d in FAR_FIRST:
        signal(third, d, 0, 0, 0)

    def far(i):
        return 2 - i + 3 * lax.div(i, 2)

    def two_lines(i):
        along_y = lax.div(i, 3)
        d = far(lax.rem(i, 3))
        dx, dy = d * (1 - along_y), d * along_y
        for dz in Z_ORDER:
            send(dx, dy, dz, 0)
        send(dx, dy, 0, 1)

    loop(6, two_lines)
    loop(9, lambda i: send(far(lax.rem(i, 3)), far(lax.div(i, 3)), 0, 0))
    pl.semaphore_wait(third, 7)

    def corner(i):
        dx, dy = far(lax.rem(i, 3)), far(lax.div(i, 3))
        for dc in (1, 0):
            for dz in Z_ORDER:
                send(dx, dy, dz, dc)
        send(dx, dy, 0, 1)

    loop(9, corner)

    def other_core(i):
        along_y = lax.div(i, 3)
        d = far(lax.rem(i, 3))
        dx, dy = d * (1 - along_y), d * along_y
        for dz in Z_ORDER:
            send(dx, dy, dz, 1)

    loop(6, other_core)
    for dz in Z_ORDER:
        send(0, 0, dz, 1)

    others = dst.at[pl.ds(0, 255)]
    pltpu.make_async_copy(others, others, recv_sem).wait()
    pltpu.make_async_copy(others, others, send_sem).wait()


def widen(arrived, restored, sums, wide, store_sem):
    def step(s, carry):
        block = arrived[pl.ds(pl.multiple_of(s * 8, 8), 8)].astype(jnp.float32).reshape(64, 1024)
        wide[s] = block
        pltpu.make_async_copy(wide.at[s], restored.at[s], store_sem).start()
        sums[s] = jnp.sum(block, axis=0)
        return carry

    lax.fori_loop(0, 32, step, 0)
    pltpu.make_async_copy(wide, restored, store_sem).wait()


def body(saved, offsets):
    arrived = pl.pallas_call(
        exchange,
        out_shape=pltpu.VMEM((256, 8, 1024), jnp.bfloat16),
        in_specs=[pl.BlockSpec(memory_space=pltpu.HBM), pl.BlockSpec(memory_space=pltpu.HBM)],
        out_specs=pl.BlockSpec(memory_space=pltpu.VMEM),
        scratch_shapes=[
            pltpu.VMEM((32, 8, 8192), jnp.bfloat16),
            pltpu.VMEM((32, 8, 8192), jnp.bfloat16),
            pltpu.SMEM((1, 32), jnp.int32),
            pltpu.SMEM((32,), jnp.int32),
            pltpu.SemaphoreType.DMA,
            pltpu.SemaphoreType.DMA,
            pltpu.SemaphoreType.DMA,
            pltpu.SemaphoreType.DMA,
            pltpu.SemaphoreType.REGULAR,
            pltpu.SemaphoreType.REGULAR,
        ],
        compiler_params=pltpu.CompilerParams(collective_id=0, has_side_effects=True, vmem_limit_bytes=62849024),
    )(saved[0], offsets)
    restored, block_sums = pl.pallas_call(
        widen,
        out_shape=(
            jax.ShapeDtypeStruct((32, 64, 1024), jnp.float32),
            jax.ShapeDtypeStruct((32, 1024), jnp.float32),
        ),
        in_specs=[pl.BlockSpec(memory_space=pltpu.VMEM)],
        out_specs=(pl.BlockSpec(memory_space=pltpu.HBM), pl.BlockSpec(memory_space=pltpu.VMEM)),
        scratch_shapes=[pltpu.VMEM((32, 64, 1024), jnp.float32), pltpu.SemaphoreType.DMA],
        compiler_params=pltpu.CompilerParams(vmem_limit_bytes=24 * MIB),
    )(arrived)
    return (restored[None], block_sums[None])


def solution(mesh):
    return jax.shard_map(
        body,
        mesh=mesh,
        in_specs=(P("section", None, "tensor", None), P("section", None)),
        out_specs=(P("section", None, None, "tensor"), P("section", None, "tensor")),
        check_vma=False,
    )
```

time: 132 us -> 105 us (0.80)
  blocking collectives: 113 us -> 0 us
  Pallas kernels: 0 us -> 104 us
  other arithmetic: 11.9 us -> 0 us
  local copies, waits for them, and re-layouts: 5.69 us -> 0 us
    all_to_all x1 -> x0, blocking collectives: 113 us -> none  [exchange_both(): parts = lax.all_to_all(parts, axis, split_axis=0, concat_axis=0, tiled=True)]
    pallas_call x0 -> x2, Pallas kernels: none -> 104 us  [the longest x1 101 us: body(): pl.pallas_call(exchange, out_shape=pltpu.VMEM((256, 8, 1024), jnp.bfloat1...]
    gather x1 -> x0, local copies, waits for them, and re-layouts: 5.02 us -> none  [body(): outgoing = jnp.take(blocks, order, axis=0)]
    convert_element_type x1 -> x0, other arithmetic: 4.47 us -> none  [body(): restored = arrived.astype(jnp.float32)]
    reduce_sum x2 -> x0, other arithmetic: 4.12 us -> none  [body(): block_sums = jnp.sum(restored, axis=1)]
    select_n x3 -> x0, other arithmetic: 3.32 us -> none  [the longest x2 2.65 us: body(): outgoing = jnp.take(blocks, order, axis=0)]
where the time goes in v1:
time: 105 us
  Pallas kernels  104 us (99%)
    pallas_call x1, Pallas kernels, body(): pl.pallas_call(exchange, out_shape=pltpu.VMEM((256, 8, 1024), jnp.bfloat1...  101 us
    pallas_call x1, Pallas kernels, body(): pl.pallas_call(widen, out_shape=(jax.ShapeDtypeStruct((32, 64, 1024), jnp...  3.93 us

profile of v1, /device:TPU:1, one launch (start us, length us, event | category | flops | bytes accessed | tf_op | source)
XLA Modules:
  0.0 105.1 jit_solution(4297517473449804318)
XLA Ops:
  0.6 100.5 %shard_map.41.arrived = bf16[256,8,1024]{2,1,0:T(8,128)(2,1)S(1)} custom-call(bf16[32,8,8192]{2,1,0:T(8,128)(2,1)} %bitcast.3, s32[1,32]{1,0:T(1,128)} %offsets.1), custom_call_target="tpu_custom_call" | custom-call | tf_op jit(solution)/shard_map/pallas_call | solution.py:143
  101.1 3.9 %shard_map.42 = (f32[32,64,1024]{2,1,0:T(8,128)}, f32[32,1024]{1,0:T(8,128)}) custom-call(bf16[256,8,1024]{2,1,0:T(8,128)(2,1)S(1)} %shard_map.41.arrived), custom_call_target="tpu_custom_call" | custom-call | tf_op jit(solution)/shard_map/pallas_call | solution.py:162

commit v2 on v1

--- a/solution.py
+++ b/solution.py
@@ -40,6 +40,10 @@
         lax.fori_loop(0, count, lambda i, carry: (step(i), carry)[1], 0)
 
     barrier = pltpu.get_barrier_semaphore()
+    read = pltpu.make_async_copy(offsets, table, table_sem)
+    read.start()
+    load = pltpu.make_async_copy(saved, raw, load_sem)
+    load.start()
     for dz in Z_ORDER:
         signal(barrier, 0, 0, dz, 0)
     for d in FAR_FIRST:
@@ -47,10 +51,6 @@
         signal(barrier, d, 0, 0, 0)
     signal(barrier, 0, 0, 0, 1)
 
-    read = pltpu.make_async_copy(offsets, table, table_sem)
-    read.start()
-    load = pltpu.make_async_copy(saved, raw, load_sem)
-    load.start()
     read.wait()
 
     def find(t):
@@ -127,16 +127,19 @@
     pltpu.make_async_copy(others, others, send_sem).wait()
 
 
-def widen(arrived, restored, sums, wide, store_sem):
+def widen(arrived, restored, sums, wide, total, store_sem, sum_sem):
     def step(s, carry):
         block = arrived[pl.ds(pl.multiple_of(s * 8, 8), 8)].astype(jnp.float32).reshape(64, 1024)
         wide[s] = block
         pltpu.make_async_copy(wide.at[s], restored.at[s], store_sem).start()
-        sums[s] = jnp.sum(block, axis=0)
+        total[s] = jnp.sum(block, axis=0)
         return carry
 
     lax.fori_loop(0, 32, step, 0)
+    written = pltpu.make_async_copy(total, sums, sum_sem)
+    written.start()
     pltpu.make_async_copy(wide, restored, store_sem).wait()
+    written.wait()
 
 
 def body(saved, offsets):
@@ -166,8 +169,13 @@
             jax.ShapeDtypeStruct((32, 1024), jnp.float32),
         ),
         in_specs=[pl.BlockSpec(memory_space=pltpu.VMEM)],
-        out_specs=(pl.BlockSpec(memory_space=pltpu.HBM), pl.BlockSpec(memory_space=pltpu.VMEM)),
-        scratch_shapes=[pltpu.VMEM((32, 64, 1024), jnp.float32), pltpu.SemaphoreType.DMA],
+        out_specs=(pl.BlockSpec(memory_space=pltpu.HBM), pl.BlockSpec(memory_space=pltpu.HBM)),
+        scratch_shapes=[
+            pltpu.VMEM((32, 64, 1024), jnp.float32),
+            pltpu.VMEM((32, 1024), jnp.float32),
+            pltpu.SemaphoreType.DMA,
+            pltpu.SemaphoreType.DMA,
+        ],
         compiler_params=pltpu.CompilerParams(vmem_limit_bytes=24 * MIB),
     )(arrived)
     return (restored[None], block_sums[None])

time: 105 us -> 105 us (level)
  no operation moved by 1% of the time
where the time goes in v2:
time: 105 us; the launch traced here: 104 us
  Pallas kernels  104 us (99%)
    pallas_call x1, Pallas kernels, body(): pl.pallas_call(exchange, out_shape=pltpu.VMEM((256, 8, 1024), jnp.bfloat1...  100 us
    pallas_call x1, Pallas kernels, body(): pl.pallas_call(widen, out_shape=(jax.ShapeDtypeStruct((32, 64, 1024), jnp...  3.32 us

profile of v2, /device:TPU:1, one launch (start us, length us, event | category | flops | bytes accessed | tf_op | source)
XLA Modules:
  0.0 104.5 jit_solution(2003589734206764624)
XLA Ops:
  0.6 100.5 %shard_map.41.arrived = bf16[256,8,1024]{2,1,0:T(8,128)(2,1)S(1)} custom-call(bf16[32,8,8192]{2,1,0:T(8,128)(2,1)} %bitcast.3, s32[1,32]{1,0:T(1,128)} %offsets.1), custom_call_target="tpu_custom_call" | custom-call | tf_op jit(solution)/shard_map/pallas_call | solution.py:146
  101.1 3.3 %shard_map.42 = (f32[32,64,1024]{2,1,0:T(8,128)}, f32[32,1024]{1,0:T(8,128)}) custom-call(bf16[256,8,1024]{2,1,0:T(8,128)(2,1)S(1)} %shard_map.41.arrived), custom_call_target="tpu_custom_call" | custom-call | tf_op jit(solution)/shard_map/pallas_call | solution.py:165
